TPU v7x, 32 devices: a whole 2x2x4 slice. The times are simulated.
32 devices in a mesh: zero: 8 (over z, x), model: 4 (over y, core).
Axes of the slice: x: 2, y: 2, z: 4, core: 2. Of those that a mesh axis runs over, the one named last changes fastest.
Arguments:
- train_up: bfloat16 [12288, 49152], P('zero', 'model'), may hold values from -0.078125 to 0.078125
- low_up: bfloat16 [12288, 32], P('zero'), may hold values from -0.0546875 to 0.0546875
- high_up: bfloat16 [32, 49152], P(None, 'model'), may hold values from -1 to 1
- norm_train: float32 [12288], P(('zero', 'model')), may hold values from 0.25 to 1.75
- norm_step: float32 [12288], P(('zero', 'model')), may hold values from -0.3 to 0.3
Outputs:
- serving_up: bfloat16 [12288, 49152], P(None, ('model', 'zero'))
- scale_up: float32 [49152], P(('model', 'zero'))
- serve_norm: bfloat16 [12288], replicated
All inputs are finite; a program needn't handle non-finite values. Where the computation divides by a largest or mean magnitude, that divisor is 1e-20 or more.
Results may differ from a plain program's by a relative error of at most 0.001.
Values may be sent and summed in bfloat16 or wider, within the bound.
A program may use at most 192 MiB of HBM per device.

v0:
```python
import jax
import jax.numpy as jnp
from jax import lax
from jax.sharding import PartitionSpec as P

D_MODEL = 12288


mix_rate = 0.5


def local(train_up, low_up, high_up, norm_train, norm_step):
    whole_up = train_up.astype(jnp.float32) + mix_rate * jnp.dot(
        low_up, high_up, preferred_element_type=jnp.float32
    )
    total_up = lax.psum(jnp.sum(jnp.abs(whole_up), axis=0), "zero")
    scale_up = total_up / D_MODEL
    narrow_up = (whole_up / scale_up).astype(jnp.bfloat16)
    serving_up = lax.all_to_all(narrow_up, "zero", split_axis=1, concat_axis=0, tiled=True)
    place = lax.axis_index("zero")
    scale_up = lax.dynamic_slice_in_dim(scale_up, place * serving_up.shape[1], serving_up.shape[1])
    serve_norm = lax.all_gather(
        (norm_train + norm_step).astype(jnp.bfloat16), ("zero", "model"), axis=0, tiled=True
    )
    return (serving_up, scale_up, serve_norm)


def solution(mesh):
    in_specs = (
        P("zero", "model"),
        P("zero", None),
        P(None, "model"),
        P(("zero", "model")),
        P(("zero", "model")),
    )
    out_specs = (P(None, ("model", "zero")), P(("model", "zero")), P())
    return jax.shard_map(local, mesh=mesh, in_specs=in_specs, out_specs=out_specs, check_vma=False)
```

profile of v0, /device:TPU:17, one launch (start us, length us, event | category | flops | bytes accessed | tf_op | source)
XLA Modules:
  0.0 1004.6 jit_solution(341893430353904681)
XLA Ops:
  0.6 0.0 copy-start
  0.6 1.1 copy-done
  1.8 38.0 %abs_reduce_fusion = (f32[12288]{0:T(1024)S(1)}, f32[1536,12288]{1,0:T(8,128)}) fusion(bf16[1536,32]{0,1:T(8,128)(2,1)} %param.6, bf16[32,12288]{1,0:T(8,128)(2,1)S(1)} %copy-done, bf16[1536,12288]{1,0:T(8,128)(2,1)} %param.5), kind=kOutput, calls=%fused_computation.1 | convolution fusion | flops 1302319104 | bytes 114180096 | tf_op jit(solution)/shard_map/dot_general | solution.py:13
  39.8 25.9 %psum.7 = f32[12288]{0:T(1024)S(1)} all-reduce(f32[12288]{0:T(1024)S(1)} %get-tuple-element.3), channel_id=1, replica_groups=mesh['zero'=8,'model'=4] {'zero'}, use_global_device_ids=true, to_apply=%region_1.0 | all-reduce | flops 12288 | bytes 98304 | tf_op jit(solution)/shard_map/psum | solution.py:16
  65.7 36.5 %divide_convert_fusion = bf16[1536,12288]{1,0:T(8,128)(2,1)} fusion(f32[1536,12288]{1,0:T(8,128)} %get-tuple-element.4, f32[12288]{0:T(1024)S(1)} %broadcast_multiply_fusion), kind=kLoop, calls=%fused_computation | loop fusion | flops 37748736 | bytes 113295360 | tf_op jit(solution)/shard_map/convert_element_type | solution.py:18
  102.2 0.0 copy-start.2
  102.2 0.0 copy-start.3
  102.2 26.0 %copy.13 = bf16[192,8,8,1536]{3,2,0,1:T(8,128)(2,1)} copy(bf16[192,8,8,1536]{3,2,1,0:T(8,128)(2,1)} %bitcast.10) | data formatting | bytes 75497472 | tf_op jit(solution)/shard_map/all_to_all | solution.py:19
  128.2 0.0 copy-start.1
  128.2 12.3 %all-to-all-start = ((bf16[1536,8,1536]{2,0,1:T(8,128)(2,1)}), bf16[1536,8,1536]{2,0,1:T(8,128)(2,1)}, u32[]{:S(2)}, u32[]{:S(2)}) async-start(bf16[1536,8,1536]{2,0,1:T(8,128)(2,1)} %bitcast.9), calls=%async_computation | async-start | bytes 75497472 | tf_op jit(solution)/shard_map/all_to_all | solution.py:19
  140.5 0.7 dynamic_slice.3
  141.1 0.0 copy-done.2
  141.1 0.0 copy-done.3
  141.2 836.7 %all-gather = bf16[32,1,384]{2,1,0:T(2,128)(2,1)S(1)} all-gather(bf16[1,1,384]{2,1,0:T(2,128)(2,1)S(1)} %reshape.10), channel_id=1, replica_groups=mesh['zero'=8,'model'=4] {'zero','model'}, dimensions={0}, use_global_device_ids=true | all-gather | bytes 25344 | tf_op jit(solution)/shard_map/all_gather | solution.py:22
  977.9 0.1 reduce
  978.0 0.6 reshape.11
  978.7 0.0 all-to-all-done
  978.7 25.9 %copy.15 = bf16[12288,1536]{1,0:T(8,128)(2,1)} copy(bf16[12288,1536]{1,0:T(8,128)(2,1)} %bitcast.1) | data formatting | bytes 75497472
  1004.6 0.0 copy-done.1
  (3 shorter events, 0.0 us)
Async XLA Ops:
  0.6 1.1 copy-start
  102.2 38.9 %copy-start.2 = (f32[384]{0:T(512)S(1)}, f32[384]{0:T(512)}, u32[]{:S(2)}) copy-start(f32[384]{0:T(512)} %param.8) | copy-start | bytes 4612
  102.2 38.9 %copy-start.3 = (f32[384]{0:T(512)S(1)}, f32[384]{0:T(512)}, u32[]{:S(2)}) copy-start(f32[384]{0:T(512)} %param.9) | copy-start | bytes 4612
  128.2 876.4 %copy-start.1 = (bf16[32,12288]{1,0:T(8,128)(2,1)S(1)}, bf16[32,12288]{1,0:T(8,128)(2,1)}, u32[]{:S(2)}) copy-start(bf16[32,12288]{1,0:T(8,128)(2,1)} %param.7) | copy-start | bytes 2359300
  128.2 850.5 %all-to-all-start = ((bf16[1536,8,1536]{2,0,1:T(8,128)(2,1)}), bf16[1536,8,1536]{2,0,1:T(8,128)(2,1)}, u32[]{:S(2)}, u32[]{:S(2)}) async-start(bf16[1536,8,1536]{2,0,1:T(8,128)(2,1)} %bitcast.9), calls=%async_computation | async-start | bytes 75497472 | tf_op jit(solution)/shard_map/all_to_all | solution.py:19
where the time goes:
time: 1000 us
  blocking collectives  863 us (86%)
  local copies, waits for them, and re-layouts  54.3 us (5%)
  matrix products  38 us (4%)
  other arithmetic  36.6 us (4%)
  starting transfers between devices  12.3 us (1%)
    all_gather x1, blocking collectives, local(): lax.all_gather((norm_train + norm_step).astype(jnp.bfloat16), ('zero', 'm...  837 us
    dot_general x1, matrix products, local(): jnp.dot(low_up, high_up, preferred_element_type=jnp.float32)  38 us
    convert_element_type x1, other arithmetic, local(): narrow_up = (whole_up / scale_up).astype(jnp.bfloat16)  36.5 us
    unnamed x11, local copies, waits for them, and re-layouts  27.7 us
    all_to_all x1, local copies, waits for them, and re-layouts, local(): lax.all_to_all(narrow_up, 'zero', split_axis=1, concat_axis=0, tiled=True)  26 us
    psum x1, blocking collectives, local(): total_up = lax.psum(jnp.sum(jnp.abs(whole_up), axis=0), 'zero')  25.9 us
  transfers between devices with their start and end apart: 1, of which 0 were waited for; matrix products, arithmetic and copies ran while one was open for 0% of the time, Pallas kernels for 0%

commit v1 on v0

v1 whole, which is shorter than its diff:
```python
import functools

import jax
import jax.numpy as jnp
from jax import lax
from jax.experimental import pallas as pl
from jax.experimental.pallas import tpu as pltpu
from jax.sharding import PartitionSpec as P

mix_rate = 0.5
PIECES = 4


def partner(me, bits, n):
    other, place = me, 1
    while place < n:
        if (bits // place) % 2:
            other = other + place * (1 - 2 * (lax.div(me, place) % 2))
        place *= 2
    return other


def send_order(n):
    far = [k for k in range(n // 2, n)]
    near = [k for k in range(n // 2 - 1, 0, -1)]
    order = []
    for i in range(len(far)):
        order.append(far[i])
        if i < len(near):
            order.append(near[i])
    return order


def exchange(n, pieces, train, low, landed, lows, own, own_low, sends, recvs, low_sends, low_recvs, mine):
    me = lax.axis_index("zero")
    rows = train.shape[0]
    cols = landed.shape[1]
    step = rows // pieces
    order = send_order(n)

    barrier = pltpu.get_barrier_semaphore()
    for k in order:
        pl.semaphore_signal(barrier, inc=1, device_id={"zero": partner(me, k, n)}, device_id_type=pl.DeviceIdType.MESH)
    pl.semaphore_wait(barrier, n - 1)

    copies = []
    for piece in range(pieces):
        for k in order:
            dest = partner(me, k, n)
            copy = pltpu.make_async_remote_copy(
                src_ref=train.at[pl.ds(piece * step, step), pl.ds(pl.multiple_of(dest * cols, 128), cols)],
                dst_ref=landed.at[pl.ds(pl.multiple_of(me * rows + piece * step, 16), step), :],
                send_sem=sends.at[k, piece],
                recv_sem=recvs.at[k, piece],
                device_id={"zero": dest},
                device_id_type=pl.DeviceIdType.MESH,
            )
            copy.start()
            copies.append(copy)
        if piece == 0:
            for k in order:
                copy = pltpu.make_async_remote_copy(
                    src_ref=low,
                    dst_ref=lows.at[me],
                    send_sem=low_sends.at[k],
                    recv_sem=low_recvs.at[k],
                    device_id={"zero": partner(me, k, n)},
                    device_id_type=pl.DeviceIdType.MESH,
                )
                copy.start()
                copies.append(copy)

    fetch = pltpu.make_async_copy(train.at[:, pl.ds(pl.multiple_of(me * cols, 128), cols)], own, mine.at[0])
    fetch_low = pltpu.make_async_copy(low, own_low, mine.at[1])
    fetch.start()
    fetch_low.start()
    fetch.wait()
    fetch_low.wait()
    keep = pltpu.make_async_copy(own, landed.at[pl.ds(pl.multiple_of(me * rows, 16), rows), :], mine.at[2])
    keep_low = pltpu.make_async_copy(own_low, lows.at[me], mine.at[3])
    keep.start()
    keep_low.start()
    keep.wait()
    keep_low.wait()
    for copy in copies:
        copy.wait()


def gather_blocks(n, train, low):
    rows, width = train.shape
    cols = width // n
    return pl.pallas_call(
        functools.partial(exchange, n, PIECES),
        out_shape=(
            jax.ShapeDtypeStruct((n * rows, cols), train.dtype),
            jax.ShapeDtypeStruct((n,) + low.shape, low.dtype),
        ),
        in_specs=[pl.BlockSpec(memory_space=pl.ANY)] * 2,
        out_specs=[pl.BlockSpec(memory_space=pl.ANY)] * 2,
        scratch_shapes=[
            pltpu.VMEM((rows, cols), train.dtype),
            pltpu.VMEM(low.shape, low.dtype),
            pltpu.SemaphoreType.DMA((n, PIECES)),
            pltpu.SemaphoreType.DMA((n, PIECES)),
            pltpu.SemaphoreType.DMA((n,)),
            pltpu.SemaphoreType.DMA((n,)),
            pltpu.SemaphoreType.DMA((4,)),
        ],
        compiler_params=pltpu.CompilerParams(collective_id=0, has_side_effects=True, vmem_limit_bytes=60 * 2**20),
        name="exchange",
    )(train, low)


def normalise(tall, landed, lows, high, serving, scale, whole):
    n, _, rows = lows.shape
    width = landed.shape[1]
    per = rows // tall
    high_tile = high[...]

    def add_up(t, total):
        i, j = lax.div(t, per), lax.rem(t, per)
        at = pl.multiple_of(t * tall, tall)
        low = lows[i, :, pl.ds(pl.multiple_of(j * tall, 128), tall)]
        extra = lax.dot_general(low, high_tile, (((0,), (0,)), ((), ())), preferred_element_type=jnp.float32)
        w = landed[pl.ds(at, tall), :].astype(jnp.float32) + extra
        whole[pl.ds(at, tall), :] = w
        return total + jnp.sum(jnp.abs(w).reshape(tall // 8, 8, width), axis=0)

    total = lax.fori_loop(0, n * per, add_up, jnp.zeros((8, width), jnp.float32), unroll=2)
    mean = jnp.sum(total, axis=0, keepdims=True) / (n * rows)
    scale[...] = mean
    inverse = 1.0 / mean

    def divide(t, carry):
        at = pl.multiple_of(t * tall, tall)
        serving[pl.ds(at, tall), :] = (whole[pl.ds(at, tall), :] * inverse).astype(serving.dtype)
        return carry

    lax.fori_loop(0, n * per, divide, 0, unroll=2)


def serve(landed, lows, high):
    height, cols = landed.shape
    n, rank, rows = lows.shape
    width = 256 if cols % 256 == 0 else 128
    tall = 256 if rows % 256 == 0 else 128
    return pl.pallas_call(
        functools.partial(normalise, tall),
        grid=(cols // width,),
        out_shape=(
            jax.ShapeDtypeStruct((height, cols), jnp.bfloat16),
            jax.ShapeDtypeStruct((1, cols), jnp.float32),
        ),
        in_specs=[
            pl.BlockSpec((height, width), lambda c: (0, c)),
            pl.BlockSpec((n, rank, rows), lambda c: (0, 0, 0)),
            pl.BlockSpec((rank, width), lambda c: (0, c)),
        ],
        out_specs=[
            pl.BlockSpec((height, width), lambda c: (0, c)),
            pl.BlockSpec((1, width), lambda c: (0, c)),
        ],
        scratch_shapes=[pltpu.VMEM((height, width), jnp.float32)],
        compiler_params=pltpu.CompilerParams(vmem_limit_bytes=60 * 2**20, dimension_semantics=("arbitrary",)),
        name="serve",
    )(landed, lows, high)


def local(n, train_up, low_up, high_up, norm_train, norm_step):
    serve_norm = lax.all_gather(
        (norm_train + norm_step).astype(jnp.bfloat16), ("zero", "model"), axis=0, tiled=True
    )
    cols = train_up.shape[1] // n
    high = lax.dynamic_slice_in_dim(high_up, lax.axis_index("zero") * cols, cols, axis=1)
    high = (mix_rate * high.astype(jnp.float32)).astype(jnp.bfloat16)
    landed, lows = gather_blocks(n, train_up, low_up.T)
    serving_up, scale_up = serve(landed, lows, high)
    return (serving_up, scale_up.reshape(-1), serve_norm)


def solution(mesh):
    in_specs = (
        P("zero", "model"),
        P("zero", None),
        P(None, "model"),
        P(("zero", "model")),
        P(("zero", "model")),
    )
    out_specs = (P(None, ("model", "zero")), P(("model", "zero")), P())
    body = functools.partial(local, mesh.shape["zero"])
    return jax.shard_map(body, mesh=mesh, in_specs=in_specs, out_specs=out_specs, check_vma=False)
```

time: 1000 us -> 928 us (0.928)
  Pallas kernels: 0 us -> 886 us
  blocking collectives: 863 us -> 33.9 us
  local copies, waits for them, and re-layouts: 54.3 us -> 0.64 us
  matrix products: 38 us -> 0 us
  other arithmetic: 36.6 us -> 3 us
  starting transfers between devices: 12.3 us -> 0 us
    pallas_call x0 -> x2, Pallas kernels: none -> 886 us  [the longest x1 836 us: gather_blocks(): pl.pallas_call(functools.partial(exchange, n, PIECES), out_shape=(jax.Sha...]
    all_gather x1, blocking collectives: 837 us -> 33.9 us  [local(): lax.all_gather((norm_train + norm_step).astype(jnp.bfloat16), ('zero', 'm...]
    dot_general x1 -> x0, matrix products: 38 us -> none  [local(): jnp.dot(low_up, high_up, preferred_element_type=jnp.float32)]
    convert_element_type x1, other arithmetic: 36.5 us -> 1.55 us  [local(): high = (mix_rate * high.astype(jnp.float32)).astype(jnp.bfloat16)]
    unnamed x11 -> x6, local copies, waits for them, and re-layouts: 27.7 us -> 0.64 us
    all_to_all x1 -> x0, local copies, waits for them, and re-layouts: 26 us -> none  [local(): lax.all_to_all(narrow_up, 'zero', split_axis=1, concat_axis=0, tiled=True)]
    psum x1 -> x0, blocking collectives: 25.9 us -> none  [local(): total_up = lax.psum(jnp.sum(jnp.abs(whole_up), axis=0), 'zero')]
    all_to_all x1 -> x0, starting transfers between devices: 12.3 us -> none  [local(): lax.all_to_all(narrow_up, 'zero', split_axis=1, concat_axis=0, tiled=True)]
  transfers between devices with their start and end apart: 1 -> 0, of which waited for: 0 -> 0; matrix products, arithmetic and copies ran while one was open for 0% -> 0% of each run, Pallas kernels for 0% -> 0%
where the time goes in v1:
time: 928 us; the launch traced here: 925 us
  Pallas kernels  886 us (95%)
  blocking collectives  33.9 us (4%)
    pallas_call x1, Pallas kernels, gather_blocks(): pl.pallas_call(functools.partial(exchange, n, PIECES), out_shape=(jax.Sha...  836 us
    pallas_call x1, Pallas kernels, serve(): pl.pallas_call(functools.partial(normalise, tall), grid=(cols // width,),...  50.6 us
    all_gather x1, blocking collectives, local(): lax.all_gather((norm_train + norm_step).astype(jnp.bfloat16), ('zero', 'm...  33.9 us

profile of v1, /device:TPU:17, one launch (start us, length us, event | category | flops | bytes accessed | tf_op | source)
XLA Modules:
  0.0 924.6 jit_solution(5549692212117763430)
XLA Ops:
  0.6 1.6 multiply_convert_fusion.high
  2.2 0.0 copy-start
  2.2 0.0 copy-start.1
  2.2 835.8 %exchange.1 = (bf16[12288,1536]{1,0:T(8,128)(2,1)}, bf16[8,32,1536]{2,1,0:T(8,128)(2,1)}) custom-call(bf16[1536,12288]{1,0:T(8,128)(2,1)} %train.1, bf16[32,1536]{1,0:T(8,128)(2,1)} %bitcast.1), custom_call_target="tpu_custom_call" | custom-call | tf_op jit(solution)/shard_map/exchange/pallas_call | solution.py:92
  838.0 50.6 %serve.1 = (bf16[12288,1536]{1,0:T(8,128)(2,1)}, f32[1,1536]{1,0:T(1,128)}) custom-call(bf16[12288,1536]{1,0:T(8,128)(2,1)} %get-tuple-element.7.landed, bf16[8,32,1536]{2,1,0:T(8,128)(2,1)} %get-tuple-element.8.lows, bf16[32,1536]{1,0:T(8,128)(2,1)} %multiply_convert_fusion.high), custom_call_target="tpu_custom_call" | custom-call | tf_op jit(solution)/shard_map/serve/pallas_call | solution.py:147
  888.7 1.3 reduce
  890.0 0.0 copy-done
  890.0 0.0 copy-done.1
  890.0 33.9 %all-gather = bf16[32,1,384]{2,1,0:T(2,128)(2,1)S(1)} all-gather(bf16[1,1,384]{2,1,0:T(2,128)(2,1)S(1)} %reshape.10), channel_id=1, replica_groups=mesh['zero'=8,'model'=4] {'zero','model'}, dimensions={0}, use_global_device_ids=true | all-gather | bytes 25344 | tf_op jit(solution)/shard_map/all_gather | solution.py:170
  923.9 0.1 reduce.1
  924.0 0.6 reshape.11
  (2 shorter events, 0.0 us)
Async XLA Ops:
  2.2 887.8 %copy-start = (f32[384]{0:T(512)S(1)}, f32[384]{0:T(512)}, u32[]{:S(2)}) copy-start(f32[384]{0:T(512)} %param.8) | copy-start | bytes 4612
  2.2 887.8 %copy-start.1 = (f32[384]{0:T(512)S(1)}, f32[384]{0:T(512)}, u32[]{:S(2)}) copy-start(f32[384]{0:T(512)} %param.9) | copy-start | bytes 4612

commit v2 on v1

--- a/solution.py
+++ b/solution.py
@@ -31,7 +31,7 @@
     return order
 
 
-def exchange(n, pieces, train, low, landed, lows, own, own_low, sends, recvs, low_sends, low_recvs, mine):
+def exchange(n, pieces, train, low, norm, landed, lows, norms, own, own_low, own_norm, sends, recvs, low_sends, low_recvs, norm_sends, norm_recvs, mine):
     me = lax.axis_index("zero")
     rows = train.shape[0]
     cols = landed.shape[1]
@@ -69,24 +69,40 @@
                 )
                 copy.start()
                 copies.append(copy)
+                copy = pltpu.make_async_remote_copy(
+                    src_ref=norm,
+                    dst_ref=norms.at[me],
+                    send_sem=norm_sends.at[k],
+                    recv_sem=norm_recvs.at[k],
+                    device_id={"zero": partner(me, k, n)},
+                    device_id_type=pl.DeviceIdType.MESH,
+                )
+                copy.start()
+                copies.append(copy)
 
     fetch = pltpu.make_async_copy(train.at[:, pl.ds(pl.multiple_of(me * cols, 128), cols)], own, mine.at[0])
     fetch_low = pltpu.make_async_copy(low, own_low, mine.at[1])
+    fetch_norm = pltpu.make_async_copy(norm, own_norm, mine.at[4])
+    fetch_norm.start()
     fetch.start()
     fetch_low.start()
     fetch.wait()
     fetch_low.wait()
+    fetch_norm.wait()
     keep = pltpu.make_async_copy(own, landed.at[pl.ds(pl.multiple_of(me * rows, 16), rows), :], mine.at[2])
     keep_low = pltpu.make_async_copy(own_low, lows.at[me], mine.at[3])
+    keep_norm = pltpu.make_async_copy(own_norm, norms.at[me], mine.at[5])
+    keep_norm.start()
     keep.start()
     keep_low.start()
     keep.wait()
     keep_low.wait()
+    keep_norm.wait()
     for copy in copies:
         copy.wait()
 
 
-def gather_blocks(n, train, low):
+def gather_blocks(n, train, low, norm):
     rows, width = train.shape
     cols = width // n
     return pl.pallas_call(
@@ -94,21 +110,25 @@
         out_shape=(
             jax.ShapeDtypeStruct((n * rows, cols), train.dtype),
             jax.ShapeDtypeStruct((n,) + low.shape, low.dtype),
+            jax.ShapeDtypeStruct((n,) + norm.shape, norm.dtype),
         ),
-        in_specs=[pl.BlockSpec(memory_space=pl.ANY)] * 2,
-        out_specs=[pl.BlockSpec(memory_space=pl.ANY)] * 2,
+        in_specs=[pl.BlockSpec(memory_space=pl.ANY)] * 3,
+        out_specs=[pl.BlockSpec(memory_space=pl.ANY)] * 3,
         scratch_shapes=[
             pltpu.VMEM((rows, cols), train.dtype),
             pltpu.VMEM(low.shape, low.dtype),
+            pltpu.VMEM(norm.shape, norm.dtype),
             pltpu.SemaphoreType.DMA((n, PIECES)),
             pltpu.SemaphoreType.DMA((n, PIECES)),
             pltpu.SemaphoreType.DMA((n,)),
             pltpu.SemaphoreType.DMA((n,)),
-            pltpu.SemaphoreType.DMA((4,)),
+            pltpu.SemaphoreType.DMA((n,)),
+            pltpu.SemaphoreType.DMA((n,)),
+            pltpu.SemaphoreType.DMA((6,)),
         ],
         compiler_params=pltpu.CompilerParams(collective_id=0, has_side_effects=True, vmem_limit_bytes=60 * 2**20),
         name="exchange",
-    )(train, low)
+    )(train, low, norm)
 
 
 def normalise(tall, landed, lows, high, serving, scale, whole):
@@ -126,7 +146,7 @@
         whole[pl.ds(at, tall), :] = w
         return total + jnp.sum(jnp.abs(w).reshape(tall // 8, 8, width), axis=0)
 
-    total = lax.fori_loop(0, n * per, add_up, jnp.zeros((8, width), jnp.float32), unroll=2)
+    total = lax.fori_loop(0, n * per, add_up, jnp.zeros((8, width), jnp.float32), unroll=4)
     mean = jnp.sum(total, axis=0, keepdims=True) / (n * rows)
     scale[...] = mean
     inverse = 1.0 / mean
@@ -167,13 +187,12 @@
 
 
 def local(n, train_up, low_up, high_up, norm_train, norm_step):
-    serve_norm = lax.all_gather(
-        (norm_train + norm_step).astype(jnp.bfloat16), ("zero", "model"), axis=0, tiled=True
-    )
+    norm = lax.all_gather(norm_train + norm_step, "model", axis=0, tiled=True).reshape(1, -1)
     cols = train_up.shape[1] // n
     high = lax.dynamic_slice_in_dim(high_up, lax.axis_index("zero") * cols, cols, axis=1)
     high = (mix_rate * high.astype(jnp.float32)).astype(jnp.bfloat16)
-    landed, lows = gather_blocks(n, train_up, low_up.T)
+    landed, lows, norms = gather_blocks(n, train_up, low_up.T, norm)
+    serve_norm = norms.reshape(-1).astype(jnp.bfloat16)
     serving_up, scale_up = serve(landed, lows, high)
     return (serving_up, scale_up.reshape(-1), serve_norm)
 

time: 928 us -> 888 us (0.957)
  blocking collectives: 33.9 us -> 6.12 us
  Pallas kernels: 886 us -> 874 us
    all_gather x1, blocking collectives: 33.9 us -> 6.12 us  [local(): lax.all_gather(norm_train + norm_step, 'model', axis=0, tiled=True)]
    pallas_call x1, Pallas kernels: 50.6 us -> 36.7 us  [serve(): pl.pallas_call(functools.partial(normalise, tall), grid=(cols // width,),...]
where the time goes in v2:
time: 888 us; the launch traced here: 885 us
  Pallas kernels  874 us (98%)
    pallas_call x1, Pallas kernels, gather_blocks(): pl.pallas_call(functools.partial(exchange, n, PIECES), out_shape=(jax.Sha...  838 us
    pallas_call x1, Pallas kernels, serve(): pl.pallas_call(functools.partial(normalise, tall), grid=(cols // width,),...  36.7 us

profile of v2, /device:TPU:17, one launch (start us, length us, event | category | flops | bytes accessed | tf_op | source)
XLA Modules:
  0.0 885.4 jit_solution(7901455681437501498)
XLA Ops:
  0.6 0.7 add.6
  1.3 6.1 all-gather
  7.5 1.5 multiply_convert_fusion.high
  9.0 837.5 %exchange.1 = (bf16[12288,1536]{1,0:T(8,128)(2,1)}, bf16[8,32,1536]{2,1,0:T(8,128)(2,1)}, f32[8,1,1536]{2,1,0:T(1,128)}) custom-call(bf16[1536,12288]{1,0:T(8,128)(2,1)} %train.1, bf16[32,1536]{1,0:T(8,128)(2,1)} %bitcast.2, f32[1,1536]{1,0:T(1,128)} %bitcast.3), custom_call_target="tpu_custom_call" | custom-call | tf_op jit(solution)/shard_map/exchange/pallas_call | solution.py:108
  846.5 0.0 copy-start
  846.6 36.7 %serve.1 = (bf16[12288,1536]{1,0:T(8,128)(2,1)}, f32[1,1536]{1,0:T(1,128)}) custom-call(bf16[12288,1536]{1,0:T(8,128)(2,1)} %get-tuple-element.8.landed, bf16[8,32,1536]{2,1,0:T(8,128)(2,1)} %get-tuple-element.9.lows, bf16[32,1536]{1,0:T(8,128)(2,1)} %multiply_convert_fusion.high), custom_call_target="tpu_custom_call" | custom-call | tf_op jit(solution)/shard_map/serve/pallas_call | solution.py:167
  883.3 1.3 reduce
  884.6 0.0 copy-done
  884.6 0.1 convert_reduce_fusion
  884.7 0.7 convert_element_type.15
  (1 shorter events, 0.0 us)
Async XLA Ops:
  846.5 38.0 %copy-start = (f32[8,1,1536]{2,1,0:T(1,128)S(1)}, f32[8,1,1536]{2,1,0:T(1,128)}, u32[]{:S(2)}) copy-start(f32[8,1,1536]{2,1,0:T(1,128)} %get-tuple-element.12) | copy-start | bytes 147460
